TPU v7x, 32 devices: a whole 2x2x4 slice. The times are simulated.
32 devices in a mesh: wide: 16 (over z, y, core), narrow: 2 (over x).
Axes of the slice: x: 2, y: 2, z: 4, core: 2. Of those that a mesh axis runs over, the one named last changes fastest.
Arguments:
- hidden_in: bfloat16 [16384, 1024], P(('wide', 'narrow')), may hold values from -6 to 6
- segment_ids: int32 [32, 512], P(('wide', 'narrow')), may hold values from 0 to 7, never falling along the last dimension, each value on 1 to 256 neighbouring positions
- expert_ids: int32 [16384, 8], P(('wide', 'narrow')), may hold values from 0 to 15, all different within a row; in each aligned block of 512 rows (0 to 511, 512 to 1023, ...) at most 512 rows name the same one
- attn_gain: float32 [1024], replicated, may hold values from 0.5 to 1.5
- w_query: bfloat16 [1024, 1024], replicated, may hold values from -0.1875 to 0.1875
- w_key: bfloat16 [1024, 512], replicated, may hold values from -0.1875 to 0.1875
- w_value: bfloat16 [1024, 512], replicated, may hold values from -0.1875 to 0.1875
- w_out: bfloat16 [1024, 1024], replicated, may hold values from -0.75 to 0.75
- ffn_gain: float32 [1024], replicated, may hold values from 0.5 to 1.5
- router: bfloat16 [1024, 16], replicated, may hold values from -0.1875 to 0.1875
- w_gate: bfloat16 [16, 1024, 512], P('wide', None, 'narrow'), may hold values from -0.1875 to 0.1875
- w_up: bfloat16 [16, 1024, 512], P('wide', None, 'narrow'), may hold values from -0.1875 to 0.1875
- w_down: bfloat16 [16, 512, 1024], P('wide', 'narrow'), may hold values from -0.75 to 0.75
- grad_out: bfloat16 [16384, 1024], P(('wide', 'narrow')), may hold values from -6 to 6
Outputs:
- hidden_out: bfloat16 [16384, 1024], P(('wide', 'narrow'))
- grad_in: bfloat16 [16384, 1024], P(('wide', 'narrow'))
- grad_attn_gain: float32 [1024], replicated
- grad_query: float32 [1024, 1024], replicated
- grad_key: float32 [1024, 512], replicated
- grad_value: float32 [1024, 512], replicated
- grad_out_proj: float32 [1024, 1024], replicated
- grad_ffn_gain: float32 [1024], replicated
- grad_router: float32 [1024, 16], replicated
- grad_gate: float32 [16, 1024, 512], P('wide', None, 'narrow')
- grad_up: float32 [16, 1024, 512], P('wide', None, 'narrow')
- grad_down: float32 [16, 512, 1024], P('wide', 'narrow')
Inputs may be any that keep to these rules, and one draw needn't show every extreme that they name: `segment_ids`: each packed row has 8 documents numbered in order from 0, each of 1 to half of 512 tokens, one of exactly half of 512. `expert_ids`: each token names 8 different experts. Among the 512 tokens of one packed row no expert is named more than 512 times, and in every draw some row names some expert exactly 512 times.
All inputs are finite; a program needn't handle non-finite values.
Results may differ from a plain program's by a relative error of at most 0.015.
Values may be sent and summed in bfloat16 or wider, within the bound.
A program may use at most 320 MiB of HBM per device.

v0:
```python
import jax
import jax.numpy as jnp
from jax import lax
from jax.sharding import PartitionSpec as P

HD = 64
EPSILON = 1e-05


def norm_scale(values):
    return lax.rsqrt(jnp.mean(values * values, axis=-1, keepdims=True) + EPSILON)


def norm_back(values, inv_rms, gain_vector, grad_rows):
    weighted = grad_rows * gain_vector
    inner = jnp.mean(weighted * values, axis=-1, keepdims=True)
    value_grad = inv_rms * weighted - values * (inv_rms * inv_rms * inv_rms) * inner
    return (value_grad, jnp.sum(grad_rows * values * inv_rms, axis=0))


def rope_tables(length, head_dim):
    half_size = head_dim // 2
    freqs = 10000.0 ** (-(jnp.arange(half_size, dtype=jnp.float32) * 2.0) / head_dim)
    angles = jnp.arange(length, dtype=jnp.float32)[:, None] * freqs[None, :]
    return (jnp.cos(angles), jnp.sin(angles))


def rotate(values, cosine_table, sine_table, direction):
    half_size = values.shape[-1] // 2
    first_half = values[..., :half_size]
    second_half = values[..., half_size:]
    cosine_part = cosine_table[:, None, :]
    sine_part = sine_table[:, None, :] * direction
    return jnp.concatenate(
        [
            first_half * cosine_part - second_half * sine_part,
            second_half * cosine_part + first_half * sine_part,
        ],
        axis=-1,
    )


def attention_probs(grouped, key_rows, allowed, head_dim):
    scores = jnp.einsum(
        "qngd,knd->ngqk", grouped, key_rows, preferred_element_type=jnp.float32
    ) * head_dim ** (-0.5)
    return jnp.where(allowed, scores, -1e30)


def on_device(
    hidden_in,
    segment_ids,
    expert_ids,
    attn_gain,
    w_query,
    w_key,
    w_value,
    w_out,
    ffn_gain,
    router,
    w_gate,
    w_up,
    w_down,
    grad_out,
):
    f32 = jnp.float32
    bf16 = jnp.bfloat16
    length, model_width = hidden_in.shape
    head_dim = HD
    head_count = w_query.shape[1] // head_dim
    kv_count = w_key.shape[1] // head_dim
    group_size = head_count // kv_count
    experts = router.shape[1]
    rows_grad = lax.all_gather(grad_out, "wide", axis=0, tiled=True)
    full_gate, full_up, full_down = (
        lax.all_gather(w_gate, "narrow", axis=2, tiled=True),
        lax.all_gather(w_up, "narrow", axis=2, tiled=True),
        lax.all_gather(w_down, "narrow", axis=1, tiled=True),
    )
    inputs = hidden_in.astype(f32)
    scale_one = norm_scale(inputs)
    normed = (inputs * scale_one * attn_gain).astype(bf16)
    query_pre = jnp.dot(normed, w_query, preferred_element_type=f32)
    key_pre = jnp.dot(normed, w_key, preferred_element_type=f32)
    value_pre = jnp.dot(normed, w_value, preferred_element_type=f32)
    cosine_table, sine_table = rope_tables(length, head_dim)
    query_rows = rotate(
        query_pre.reshape(length, head_count, head_dim), cosine_table, sine_table, 1.0
    ).astype(bf16)
    key_rows = rotate(
        key_pre.reshape(length, kv_count, head_dim), cosine_table, sine_table, 1.0
    ).astype(bf16)
    value_rows = value_pre.astype(bf16).reshape(length, kv_count, head_dim)
    grouped = query_rows.reshape(length, kv_count, group_size, head_dim)
    segments = segment_ids[0]
    places = jnp.arange(length, dtype=jnp.int32)
    allowed = (segments[:, None] == segments[None, :]) & (places[:, None] >= places[None, :])
    scores = attention_probs(grouped, key_rows, allowed, head_dim)
    row_max = jnp.max(scores, axis=-1, keepdims=True)
    log_total = row_max + jnp.log(jnp.sum(jnp.exp(scores - row_max), axis=-1, keepdims=True))
    weights_prob = jnp.exp(scores - log_total)
    attended = jnp.einsum(
        "ngqk,knd->qngd", weights_prob.astype(bf16), value_rows, preferred_element_type=f32
    )
    attended = attended.reshape(length, head_count * head_dim).astype(bf16)
    mixed_rows = inputs + jnp.dot(attended, w_out, preferred_element_type=f32)
    scale_two = norm_scale(mixed_rows)
    ffn_normed = (mixed_rows * scale_two * ffn_gain).astype(bf16)
    logits = jnp.dot(ffn_normed, router, preferred_element_type=f32)
    picked = expert_ids[:, :, None] == jnp.arange(experts, dtype=jnp.int32)[None, None, :]
    member = jnp.any(picked, axis=1)
    masked = jnp.where(member, logits, -jnp.inf)
    powers = jnp.where(member, jnp.exp(masked - jnp.max(masked, axis=-1, keepdims=True)), 0.0)
    gate_probs = powers / jnp.sum(powers, axis=-1, keepdims=True)
    row_gates = lax.all_to_all(gate_probs.T, "wide", split_axis=0, concat_axis=0, tiled=True)
    row_gates = row_gates.reshape(-1, 1)
    rows_in = lax.all_gather(ffn_normed, "wide", axis=0, tiled=True)
    gate_act = jnp.dot(rows_in, full_gate[0], preferred_element_type=f32)
    up_act = jnp.dot(rows_in, full_up[0], preferred_element_type=f32)
    hidden_act = (jax.nn.silu(gate_act) * up_act).astype(bf16)
    outputs = jnp.dot(hidden_act, full_down[0], preferred_element_type=f32).astype(bf16)
    moe_rows = lax.psum_scatter(
        (row_gates * outputs.astype(f32)).astype(bf16), "wide", scatter_dimension=0, tiled=True
    )
    hidden_out = (mixed_rows + moe_rows.astype(f32)).astype(bf16)
    cotangent = grad_out.astype(f32)
    gate_dots = jnp.sum(outputs.astype(f32) * rows_grad.astype(f32), axis=-1)
    gate_grads = lax.all_to_all(
        gate_dots.reshape(experts, length), "wide", split_axis=0, concat_axis=0, tiled=True
    ).T
    logit_grads = (
        gate_probs * (gate_grads - jnp.sum(gate_probs * gate_grads, axis=-1, keepdims=True))
    ).astype(bf16)
    router_grad = jnp.einsum("sd,se->de", ffn_normed, logit_grads, preferred_element_type=f32)
    normed_two_grad = jnp.einsum("se,de->sd", logit_grads, router, preferred_element_type=f32)
    grads_in = (row_gates * rows_grad.astype(f32)).astype(bf16)
    hidden_grad = jnp.einsum("rd,fd->rf", grads_in, full_down[0], preferred_element_type=f32)
    down_w_grad = jnp.einsum("rf,rd->fd", hidden_act, grads_in, preferred_element_type=f32)
    sigmoid_gate = jax.nn.sigmoid(gate_act)
    gate_grad = (
        hidden_grad * up_act * sigmoid_gate * (1.0 + gate_act * (1.0 - sigmoid_gate))
    ).astype(bf16)
    up_grad = (hidden_grad * gate_act * sigmoid_gate).astype(bf16)
    gate_w_grad = jnp.einsum("rd,rf->df", rows_in, gate_grad, preferred_element_type=f32)
    up_w_grad = jnp.einsum("rd,rf->df", rows_in, up_grad, preferred_element_type=f32)
    copy_grads = (
        jnp.einsum("rf,df->rd", gate_grad, full_gate[0], preferred_element_type=f32)
        + jnp.einsum("rf,df->rd", up_grad, full_up[0], preferred_element_type=f32)
    ).astype(bf16)
    rows_back = lax.psum_scatter(copy_grads, "wide", scatter_dimension=0, tiled=True)
    gate_w_grad, up_w_grad, down_w_grad = (
        lax.psum_scatter(
            gate_w_grad[None].astype(jnp.bfloat16), "narrow", scatter_dimension=2, tiled=True
        ).astype(jnp.float32),
        lax.psum_scatter(
            up_w_grad[None].astype(jnp.bfloat16), "narrow", scatter_dimension=2, tiled=True
        ).astype(jnp.float32),
        lax.psum_scatter(
            down_w_grad[None].astype(jnp.bfloat16), "narrow", scatter_dimension=1, tiled=True
        ).astype(jnp.float32),
    )
    normed_two_grad = normed_two_grad + rows_back.astype(f32)
    mixed_part, ffn_gain_grad = norm_back(mixed_rows, scale_two, ffn_gain, normed_two_grad)
    mixed_grad = cotangent + mixed_part
    branch_grad = mixed_grad.astype(bf16)
    out_w_grad = jnp.einsum("sh,sd->hd", attended, branch_grad, preferred_element_type=f32)
    attended_grad = jnp.einsum("sd,hd->sh", branch_grad, w_out, preferred_element_type=f32).astype(
        bf16
    )
    attended_grad = attended_grad.reshape(length, kv_count, group_size, head_dim)
    scores = attention_probs(grouped, key_rows, allowed, head_dim)
    weights_prob = jnp.exp(scores - log_total)
    value_grad = jnp.einsum(
        "ngqk,qngd->knd", weights_prob.astype(bf16), attended_grad, preferred_element_type=f32
    )
    prob_grad = jnp.einsum("qngd,knd->ngqk", attended_grad, value_rows, preferred_element_type=f32)
    score_grad = (
        weights_prob * (prob_grad - jnp.sum(weights_prob * prob_grad, axis=-1, keepdims=True))
    ).astype(bf16)
    query_grad = jnp.einsum(
        "ngqk,knd->qngd", score_grad, key_rows, preferred_element_type=f32
    ) * head_dim ** (-0.5)
    key_grad = jnp.einsum(
        "ngqk,qngd->knd", score_grad, grouped, preferred_element_type=f32
    ) * head_dim ** (-0.5)
    query_grad = rotate(
        query_grad.reshape(length, head_count, head_dim), cosine_table, sine_table, -1.0
    )
    query_grad = query_grad.reshape(length, -1).astype(bf16)
    key_grad = rotate(key_grad, cosine_table, sine_table, -1.0).reshape(length, -1).astype(bf16)
    value_grad = value_grad.reshape(length, -1).astype(bf16)
    query_w_grad = jnp.einsum("sd,sh->dh", normed, query_grad, preferred_element_type=f32)
    key_w_grad = jnp.einsum("sd,sh->dh", normed, key_grad, preferred_element_type=f32)
    value_w_grad = jnp.einsum("sd,sh->dh", normed, value_grad, preferred_element_type=f32)
    normed_one_grad = (
        jnp.einsum("sh,dh->sd", query_grad, w_query, preferred_element_type=f32)
        + jnp.einsum("sh,dh->sd", key_grad, w_key, preferred_element_type=f32)
        + jnp.einsum("sh,dh->sd", value_grad, w_value, preferred_element_type=f32)
    )
    input_part, attn_gain_grad = norm_back(inputs, scale_one, attn_gain, normed_one_grad)
    grad_in = (mixed_grad + input_part).astype(bf16)
    small = jnp.concatenate(
        [
            attn_gain_grad.reshape(-1, 128),
            ffn_gain_grad.reshape(-1, 128),
            router_grad.reshape(-1, 128),
        ],
        axis=0,
    )
    everywhere = ("wide", "narrow")
    columns = jnp.concatenate([query_w_grad, key_w_grad, value_w_grad, out_w_grad], axis=1)
    shares = lax.psum_scatter(columns.astype(bf16), everywhere, scatter_dimension=0, tiled=True)
    columns = lax.all_gather(shares, everywhere, axis=0, tiled=True).astype(f32)
    small = lax.psum(small, everywhere)
    gain_rows = model_width // 128
    query_width, key_width = (w_query.shape[1], w_key.shape[1])
    summed = (
        small[:gain_rows].reshape(-1),
        columns[:, :query_width],
        columns[:, query_width : query_width + key_width],
        columns[:, query_width + key_width : query_width + 2 * key_width],
        columns[:, query_width + 2 * key_width :],
        small[gain_rows : 2 * gain_rows].reshape(-1),
        small[2 * gain_rows :].reshape(router.shape),
    )
    return (
        hidden_out,
        grad_in,
        summed[0],
        summed[1],
        summed[2],
        summed[3],
        summed[4],
        summed[5],
        summed[6],
        gate_w_grad,
        up_w_grad,
        down_w_grad,
    )


def solution(mesh):
    return jax.shard_map(
        on_device,
        mesh=mesh,
        in_specs=(
            P(("wide", "narrow"), None),
            P(("wide", "narrow"), None),
            P(("wide", "narrow"), None),
            P(),
            P(),
            P(),
            P(),
            P(),
            P(),
            P(),
            P("wide", None, "narrow"),
            P("wide", None, "narrow"),
            P("wide", "narrow", None),
            P(("wide", "narrow"), None),
        ),
        out_specs=(
            P(("wide", "narrow"), None),
            P(("wide", "narrow"), None),
            P(),
            P(),
            P(),
            P(),
            P(),
            P(),
            P(),
            P("wide", None, "narrow"),
            P("wide", None, "narrow"),
            P("wide", "narrow", None),
        ),
        check_vma=False,
    )
```

profile of v0, /device:TPU:0, one launch (start us, length us, event | category | flops | bytes accessed | tf_op | source)
XLA Modules:
  0.0 1261.6 jit_solution(9160530426510023094)
XLA Ops:
  17.5 7.8 fusion.83
  25.3 8.2 exponential_reduce_fusion
  33.6 8.5 fusion.25
  51.5 7.3 all-to-all-start
  58.9 116.9 %all-gather.7.cloned.1.call-done = bf16[8192,1024]{1,0:T(8,128)(2,1)} async-done(((bf16[512,1024]{1,0:T(8,128)(2,1)}), bf16[8192,1024]{1,0:T(8,128)(2,1)}) %all-gather.7.cloned.1.call-update) | async-done | bytes 16777232 | tf_op jit(solution)/shard_map/all_gather | solution.py:117
  175.9 16.5 %fusion.47 = f32[8192,512]{1,0:T(8,128)} fusion(bf16[8192,1024]{1,0:T(8,128)(2,1)} %all-gather.7.cloned.1.call-done, bf16[1,1024,512]{2,1,0:T(8,128)(2,1)} %all-gather.11.cloned.1.call-done), kind=kOutput, calls=%fused_computation.74 | convolution fusion | flops 8589934592 | bytes 34603008 | tf_op jit(solution)/shard_map/dot_general | solution.py:119
  192.4 4.5 all-gather.9.cloned.1.call-done
  196.9 16.0 %fusion.51 = f32[8192,512]{1,0:T(8,128)} fusion(bf16[8192,1024]{1,0:T(8,128)(2,1)} %all-gather.7.cloned.1.call-done, bf16[1,1024,512]{2,1,0:T(8,128)(2,1)} %all-gather.9.cloned.1.call-done), kind=kOutput, calls=%fused_computation.78 | convolution fusion | flops 8589934592 | bytes 34603008 | tf_op jit(solution)/shard_map/dot_general | solution.py:118
  212.8 6.7 all-gather.13.cloned.1.call-done
  219.6 128.5 %all-gather.15.cloned.1.call-done = bf16[8192,1024]{1,0:T(8,128)(2,1)} async-done(((bf16[512,1024]{1,0:T(8,128)(2,1)}), bf16[8192,1024]{1,0:T(8,128)(2,1)}) %all-gather.15.cloned.1.call-update) | async-done | bytes 16777232 | tf_op jit(solution)/shard_map/all_gather | solution.py:74
  348.1 32.2 %multiply_convert_fusion = (bf16[8192,512]{1,0:T(8,128)(2,1)}, bf16[8192,512]{1,0:T(8,128)(2,1)}, bf16[8192,512]{1,0:T(8,128)(2,1)}) fusion(f32[8192,512]{1,0:T(8,128)} %fusion.51, f32[8192,512]{1,0:T(8,128)} %fusion.47, bf16[1,512,1024]{2,1,0:T(8,128)(2,1)} %all-gather.13.cloned.1.call-done, bf16[8192,1024]{1,0:T(8,128)(2,1)} %all-gather.15.cloned.1.call-done, ...), kind=kOutput, calls=%fused_computation.13 | convolution fusion | flops 8682209280 | bytes 76578816 | tf_op jit(solution)/shard_map/rd,fd->rf/dot_general | solution.py:137
  380.3 18.8 %fusion.49 = f32[8192,1024]{1,0:T(8,128)} fusion(bf16[8192,512]{1,0:T(8,128)(2,1)} %get-tuple-element.65, bf16[1,1024,512]{2,1,0:T(8,128)(2,1)S(1)} %copy-done.62), kind=kOutput, calls=%fused_computation.76 | convolution fusion | flops 8589934592 | bytes 42991616 | tf_op jit(solution)/shard_map/rf,df->rd/dot_general | solution.py:147
  399.1 21.5 %add_convert_fusion = bf16[8192,1024]{1,0:T(8,128)(2,1)} fusion(f32[8192,1024]{1,0:T(8,128)} %fusion.49, bf16[8192,512]{1,0:T(8,128)(2,1)} %get-tuple-element.64, bf16[1,1024,512]{2,1,0:T(8,128)(2,1)S(1)} %copy-done.60), kind=kOutput, calls=%fused_computation.6 | convolution fusion | flops 8606711808 | bytes 59768832 | tf_op jit(solution)/shard_map/rf,df->rd/dot_general | solution.py:148
  421.9 23.7 %fusion.1 = (f32[8192]{0:T(1024)S(1)}, bf16[8192,1024]{1,0:T(8,128)(2,1)}) fusion(bf16[8192,1024]{1,0:T(8,128)(2,1)} %all-gather.15.cloned.1.call-done, f32[8192]{0:T(1024)S(1)} %bitcast.185, bf16[8192,512]{1,0:T(8,128)(2,1)} %get-tuple-element.66, bf16[1,512,1024]{2,1,0:T(8,128)(2,1)S(1)} %copy-done.61), kind=kOutput, calls=%fused_computation.4 | convolution fusion | flops 8648646656 | bytes 43057152 | tf_op jit(solution)/shard_map/dot_general | solution.py:121
  445.7 9.3 all_to_all.21
  455.1 141.1 %reduce-scatter.11.cloned.1.call-done = bf16[512,1024]{1,0:T(8,128)(2,1)} async-done(((bf16[8192,1024]{1,0:T(8,128)(2,1)}), bf16[512,1024]{1,0:T(8,128)(2,1)}) %reduce-scatter.11.cloned.1.call-update) | async-done | bytes 1048592 | tf_op jit(solution)/shard_map/reduce_scatter | solution.py:150
  600.2 176.6 %reduce-scatter.9.cloned.1.call-done = bf16[512,1024]{1,0:T(8,128)(2,1)} async-done(((bf16[8192,1024]{1,0:T(8,128)(2,1)}), bf16[512,1024]{1,0:T(8,128)(2,1)}) %reduce-scatter.9.cloned.1.call-update) | async-done | bytes 1048592 | tf_op jit(solution)/shard_map/reduce_scatter | solution.py:122
  788.5 9.4 fusion.41
  797.9 16.0 %fusion.3 = (f32[8,2,512]{2,1,0:T(2,128)}, f32[8,512,512,2]{2,1,3,0:T(8,128)}) fusion(f32[8,2,512,512]{2,3,1,0:T(8,128)} %get-tuple-element.93, f32[8,2,512]{2,1,0:T(2,128)S(1)} %bitcast.181, bf16[512,8,64,1]{0,2,3,1:T(8,128)(2,1)} %bitcast.165, bf16[512,8,2,64]{0,3,2,1:T(8,128)(2,1)} %bitcast.160), kind=kOutput, calls=%fused_computation.9 | convolution fusion | flops 549445632 | bytes 35192832 | tf_op jit(solution)/shard_map/qngd,knd->ngqk/dot_general | solution.py:176
  814.0 11.1 fusion.5
  825.1 6.3 fusion.37
  838.8 15.2 %pad_maximum_fusion = bf16[1024,3072]{0,1:T(8,128)(2,1)} fusion(bf16[1024,1024]{0,1:T(8,128)(2,1)S(1)} %copy-done.20, bf16[1024,512]{0,1:T(8,128)(2,1)S(1)} %convolution_convert_fusion.6, bf16[1024,512]{0,1:T(8,128)(2,1)S(1)} %convolution_convert_fusion.7, bf16[1024,1024]{0,1:T(8,128)(2,1)S(1)} %convolution_convert_fusion.1), kind=kLoop, calls=%fused_computation.23 | loop fusion | flops 25165824 | bytes 12582912 | tf_op jit(solution)/shard_map/concatenate | solution.py:211
  854.0 8.7 copy.93
  862.7 15.7 %fusion.32 = bf16[1,1024,512]{2,1,0:T(8,128)(2,1)} fusion(bf16[8192,1024]{1,0:T(8,128)(2,1)} %all-gather.7.cloned.1.call-done, bf16[8192,512]{1,0:T(8,128)(2,1)} %get-tuple-element.64), kind=kOutput, calls=%fused_computation.61 | convolution fusion | flops 8590458880 | bytes 26214400 | tf_op jit(solution)/shard_map/rd,rf->df/dot_general | solution.py:145
  878.5 16.1 %fusion.31 = bf16[1,1024,512]{2,1,0:T(8,128)(2,1)} fusion(bf16[8192,1024]{1,0:T(8,128)(2,1)} %all-gather.7.cloned.1.call-done, bf16[8192,512]{1,0:T(8,128)(2,1)} %get-tuple-element.65), kind=kOutput, calls=%fused_computation.60 | convolution fusion | flops 8590458880 | bytes 26214400 | tf_op jit(solution)/shard_map/rd,rf->df/dot_general | solution.py:144
  895.0 18.9 %fusion.38 = bf16[1,512,1024]{2,1,0:T(8,128)(2,1)} fusion(bf16[8192,512]{1,0:T(8,128)(2,1)} %get-tuple-element.66, bf16[8192,1024]{1,0:T(8,128)(2,1)} %all-gather.15.cloned.1.call-done, f32[8192]{0:T(1024)S(1)} %bitcast.186), kind=kOutput, calls=%fused_computation.66 | convolution fusion | flops 8615624704 | bytes 26247168 | tf_op jit(solution)/shard_map/rf,rd->fd/dot_general | solution.py:138
  925.6 51.4 %reduce-scatter.19.cloned.1.call-done = bf16[32,3072]{1,0:T(8,128)(2,1)} async-done(((bf16[1024,3072]{1,0:T(8,128)(2,1)}), bf16[32,3072]{1,0:T(8,128)(2,1)}) %reduce-scatter.19.cloned.1.call-update) | async-done | bytes 196624 | tf_op jit(solution)/shard_map/reduce_scatter | solution.py:212
  976.9 22.2 %reduce-scatter.15.cloned.1.call-done = bf16[1,1024,256]{2,1,0:T(8,128)(2,1)} async-done(((bf16[1,1024,512]{2,1,0:T(8,128)(2,1)}), bf16[1,1024,256]{2,1,0:T(8,128)(2,1)}) %reduce-scatter.15.cloned.1.call-update) | async-done | bytes 524304 | tf_op jit(solution)/shard_map/reduce_scatter | solution.py:155
  1001.2 21.0 %reduce-scatter.13.cloned.1.call-done = bf16[1,1024,256]{2,1,0:T(8,128)(2,1)} async-done(((bf16[1,1024,512]{2,1,0:T(8,128)(2,1)}), bf16[1,1024,256]{2,1,0:T(8,128)(2,1)}) %reduce-scatter.13.cloned.1.call-update) | async-done | bytes 524304 | tf_op jit(solution)/shard_map/reduce_scatter | solution.py:152
  1024.3 21.2 %reduce-scatter.17.cloned.1.call-done = bf16[1,256,1024]{2,1,0:T(8,128)(2,1)} async-done(((bf16[1,512,1024]{2,1,0:T(8,128)(2,1)}), bf16[1,256,1024]{2,1,0:T(8,128)(2,1)}) %reduce-scatter.17.cloned.1.call-update) | async-done | bytes 524304 | tf_op jit(solution)/shard_map/reduce_scatter | solution.py:158
  1051.4 120.4 %all-reduce.2.cloned.1.call-done = f32[144,128]{1,0:T(8,128)} async-done(((f32[144,128]{1,0:T(8,128)}), f32[144,128]{1,0:T(8,128)}) %all-reduce.2.cloned.1.call-update) | async-done | bytes 73744 | tf_op jit(solution)/shard_map/psum | solution.py:214
  1174.9 71.2 %all-gather.17.cloned.1.call-done = bf16[1024,3072]{1,0:T(8,128)(2,1)} async-done(((bf16[32,3072]{1,0:T(8,128)(2,1)}), bf16[1024,3072]{1,0:T(8,128)(2,1)}) %all-gather.17.cloned.1.call-update) | async-done | bytes 6291472 | tf_op jit(solution)/shard_map/all_gather | solution.py:213
  (214 shorter events, 77.5 us)
Async XLA Ops:
  7.2 34.9 %copy-start = (bf16[1024,1024]{1,0:T(8,128)(2,1)S(1)}, bf16[1024,1024]{1,0:T(8,128)(2,1)}, u32[]{:S(2)}) copy-start(bf16[1024,1024]{1,0:T(8,128)(2,1)} %param.21) | copy-start | bytes 6291460
  7.2 51.7 %all-gather.11.cloned.1.call-start = ((), (), s32[]{:S(2)}) async-start(), calls=%async_computation.10 | async-start | bytes 1572864 | tf_op jit(solution)/shard_map/all_gather | solution.py:77
  8.0 167.9 %all-gather.7.cloned.1.call-start = ((), (), s32[]{:S(2)}) async-start(), calls=%async_computation.8 | async-start | bytes 17825792 | tf_op jit(solution)/shard_map/all_gather | solution.py:117
  14.6 19.0 %copy-start.13 = (bf16[512,512]{0,1:T(8,128)(2,1)}, bf16[512,512]{0,1:T(8,128)(2,1)S(1)}, u32[]{:S(2)}) copy-start(bf16[512,512]{0,1:T(8,128)(2,1)S(1)} %convolution_convert_fusion.8) | copy-start | bytes 1572868
  46.1 150.8 %all-gather.9.cloned.1.call-start = ((), (), s32[]{:S(2)}) async-start(), calls=%async_computation.9 | async-start | bytes 1572864 | tf_op jit(solution)/shard_map/all_gather | solution.py:76
  46.8 172.8 %all-gather.13.cloned.1.call-start = ((), (), s32[]{:S(2)}) async-start(), calls=%async_computation.11 | async-start | bytes 1572864 | tf_op jit(solution)/shard_map/all_gather | solution.py:78
  47.4 300.7 %all-gather.15.cloned.1.call-start = ((), (), s32[]{:S(2)}) async-start(), calls=%async_computation.13 | async-start | bytes 17825792 | tf_op jit(solution)/shard_map/all_gather | solution.py:74
  51.5 161.3 %all-to-all-start = ((f32[16,1,512]{2,1,0:T(1,128)}), f32[16,1,512]{2,1,0:T(1,128)S(1)}, u32[]{:S(2)}, u32[]{:S(2)}) async-start(f32[16,1,512]{2,1,0:T(1,128)} %copy.73), calls=%async_computation | async-start | bytes 65536 | tf_op jit(solution)/shard_map/all_to_all | solution.py:115
  58.9 537.4 %reduce-scatter.11.cloned.1.call-start = ((), (), s32[]{:S(2)}) async-start(), calls=%async_computation.14 | async-start | bytes 17825792 | tf_op jit(solution)/shard_map/reduce_scatter | solution.py:150
  212.8 207.9 %copy-start.50 = (f32[16,1,512]{2,1,0:T(1,128)}, f32[16,1,512]{2,1,0:T(1,128)S(1)}, u32[]{:S(2)}) copy-start(f32[16,1,512]{2,1,0:T(1,128)S(1)} %all-to-all-done) | copy-start | bytes 98308
  348.1 32.2 %copy-start.62 = (bf16[1,1024,512]{2,1,0:T(8,128)(2,1)S(1)}, bf16[1,1024,512]{2,1,0:T(8,128)(2,1)}, u32[]{:S(2)}) copy-start(bf16[1,1024,512]{2,1,0:T(8,128)(2,1)} %all-gather.9.cloned.1.call-done) | copy-start | bytes 3145732
  380.3 18.8 %copy-start.60 = (bf16[1,1024,512]{2,1,0:T(8,128)(2,1)S(1)}, bf16[1,1024,512]{2,1,0:T(8,128)(2,1)}, u32[]{:S(2)}) copy-start(bf16[1,1024,512]{2,1,0:T(8,128)(2,1)} %all-gather.11.cloned.1.call-done) | copy-start | bytes 3145732
  420.7 356.2 %reduce-scatter.9.cloned.1.call-start = ((), (), s32[]{:S(2)}) async-start(), calls=%async_computation.12 | async-start | bytes 17825792 | tf_op jit(solution)/shard_map/reduce_scatter | solution.py:122
  445.6 150.7 %copy-start.41 = (bf16[1024,16]{0,1:T(8,128)(2,1)S(1)}, bf16[1024,16]{0,1:T(8,128)(2,1)}, u32[]{:S(2)}) copy-start(bf16[1024,16]{0,1:T(8,128)(2,1)} %param.23) | copy-start | bytes 98308
  445.6 150.7 %copy-start.47 = (f32[1024]{0:T(1024)S(1)}, f32[1024]{0:T(1024)}, u32[]{:S(2)}) copy-start(f32[1024]{0:T(1024)} %param.22) | copy-start | bytes 12292
  445.6 150.7 %copy-start.49 = (f32[512]{0:T(512)S(1)}, f32[512]{0:T(512)}, u32[]{:S(2)}) copy-start(f32[512]{0:T(512)} %copy-done.48) | copy-start | bytes 6148
  445.7 331.2 %copy-start.10 = (bf16[512,1024]{1,0:T(8,128)(2,1)S(1)}, bf16[512,1024]{1,0:T(8,128)(2,1)}, u32[]{:S(2)}) copy-start(bf16[512,1024]{1,0:T(8,128)(2,1)} %param.27) | copy-start | bytes 3145732
  445.7 331.2 %copy-start.58 = (f32[512]{0:T(512)S(1)}, f32[512]{0:T(512)}, u32[]{:S(2)}) copy-start(f32[512]{0:T(512)} %get-tuple-element.87) | copy-start | bytes 6148
  445.7 531.2 %reduce-scatter.19.cloned.1.call-start = ((), (), s32[]{:S(2)}) async-start(), calls=%async_computation.20 | async-start | bytes 6488064 | tf_op jit(solution)/shard_map/reduce_scatter | solution.py:212
  455.1 326.0 %copy-start.36 = (f32[16,1,512]{2,1,0:T(1,128)}, f32[16,1,512]{2,1,0:T(1,128)S(1)}, u32[]{:S(2)}) copy-start(f32[16,1,512]{2,1,0:T(1,128)S(1)} %all_to_all.21) | copy-start | bytes 98308
  788.5 25.4 %slice-start = ((s8[16777216]{0:T(1024)(128)(4,1)}), s8[4194304]{0:T(1024)(128)(4,1)S(1)}, s32[]{:S(2)}) async-start(s8[16777216]{0:T(1024)(128)(4,1)} %bitcast.157), calls=%async_computation.21 | async-start | bytes 8388608
  788.5 25.4 %slice-start.1 = ((s8[16777216]{0:T(1024)(128)(4,1)}), s8[4194304]{0:T(1024)(128)(4,1)S(1)}, s32[]{:S(2)}) async-start(s8[16777216]{0:T(1024)(128)(4,1)} %bitcast.157), calls=%async_computation.22 | async-start | bytes 8388608
  862.7 136.5 %reduce-scatter.15.cloned.1.call-start = ((), (), s32[]{:S(2)}) async-start(), calls=%async_computation.18 | async-start | bytes 1572864 | tf_op jit(solution)/shard_map/reduce_scatter | solution.py:155
  878.5 16.5 %copy-start.51 = (f32[16,1,512]{2,1,0:T(1,128)S(1)}, f32[16,1,512]{2,1,0:T(1,128)}, u32[]{:S(2)}) copy-start(f32[16,1,512]{2,1,0:T(1,128)} %copy-done.50) | copy-start | bytes 98308
  878.5 143.7 %reduce-scatter.13.cloned.1.call-start = ((), (), s32[]{:S(2)}) async-start(), calls=%async_computation.17 | async-start | bytes 1572864 | tf_op jit(solution)/shard_map/reduce_scatter | solution.py:152
  894.7 19.2 %copy-start.4 = (bf16[512,1024]{1,0:T(8,128)(2,1)S(1)}, bf16[512,1024]{1,0:T(8,128)(2,1)}, u32[]{:S(2)}) copy-start(bf16[512,1024]{1,0:T(8,128)(2,1)} %multiply_convert_fusion.3) | copy-start | bytes 3145732
  894.7 19.2 %copy-start.25 = (f32[512,16]{0,1:T(8,128)S(1)}, f32[512,16]{0,1:T(8,128)}, u32[]{:S(2)}) copy-start(f32[512,16]{0,1:T(8,128)} %copy-done.23) | copy-start | bytes 98308
  894.7 19.2 %copy-start.37 = (f32[16,1,512]{2,1,0:T(1,128)S(1)}, f32[16,1,512]{2,1,0:T(1,128)}, u32[]{:S(2)}) copy-start(f32[16,1,512]{2,1,0:T(1,128)} %copy-done.36) | copy-start | bytes 98308
  894.7 150.8 %reduce-scatter.17.cloned.1.call-start = ((), (), s32[]{:S(2)}) async-start(), calls=%async_computation.19 | async-start | bytes 1572864 | tf_op jit(solution)/shard_map/reduce_scatter | solution.py:158
  913.9 257.9 %all-reduce.2.cloned.1.call-start = ((), (), s32[]{:S(2)}) async-start(), calls=%async_computation.15 | async-start | bytes 147456 | tf_op jit(solution)/shard_map/psum | solution.py:214
  924.6 123.0 %copy-start.57 = (f32[512]{0:T(512)S(1)}, f32[512]{0:T(512)}, u32[]{:S(2)}) copy-start(f32[512]{0:T(512)} %get-tuple-element.85) | copy-start | bytes 6148
  925.3 320.8 %all-gather.17.cloned.1.call-start = ((), (), s32[]{:S(2)}) async-start(), calls=%async_computation.16 | async-start | bytes 6488064 | tf_op jit(solution)/shard_map/all_gather | solution.py:213
  (49 other events, 242.6 us)
Sparse Core Ops, SparseCore 0:
  9.6 23.9 all-gather.10
  46.2 129.6 all-gather.6
  177.4 19.4 all-gather.8
  198.3 21.2 all-gather.12
  221.6 126.4 all-gather.14
  420.8 175.4 reduce-scatter.10
  600.4 176.4 reduce-scatter.8
  862.8 114.0 reduce-scatter.18
  979.7 19.3 reduce-scatter.14
  1001.8 20.3 reduce-scatter.12
  1025.0 20.3 reduce-scatter.16
  1051.5 120.2 all-reduce.1
  1174.7 71.3 all-gather.16
where the time goes:
time: 1270 us; the launch traced here: 1260 us
  waiting for transfers between devices  884 us (70%)
  matrix products  258 us (20%)
  other arithmetic  56.7 us (4%)
  local copies, waits for them, and re-layouts  30 us (2%)
  between operations  15.1 us (1%)
    reduce_scatter x1, waiting for transfers between devices, on_device(): lax.psum_scatter((row_gates * outputs.astype(f32)).astype(bf16), 'wide',...  177 us
    reduce_scatter x1, waiting for transfers between devices, on_device(): lax.psum_scatter(copy_grads, 'wide', scatter_dimension=0, tiled=True)  141 us
    all_gather x1, waiting for transfers between devices, on_device(): rows_grad = lax.all_gather(grad_out, 'wide', axis=0, tiled=True)  128 us
    psum x1, waiting for transfers between devices, on_device(): small = lax.psum(small, everywhere)  120 us
    all_gather x1, waiting for transfers between devices, on_device(): rows_in = lax.all_gather(ffn_normed, 'wide', axis=0, tiled=True)  117 us
    all_gather x1, waiting for transfers between devices, on_device(): columns = lax.all_gather(shares, everywhere, axis=0, tiled=True).astype(f32)  71.2 us
    reduce_scatter x1, waiting for transfers between devices, on_device(): lax.psum_scatter(columns.astype(bf16), everywhere, scatter_dimension=0, t...  51.4 us
    dot_general x1, matrix products, on_device(): jnp.einsum('rd,fd->rf', grads_in, full_down[0], preferred_element_type=f32)  32.2 us
  transfers between devices with their start and end apart: 14, of which 12 were waited for; matrix products, arithmetic and copies ran while one was open for 14% of the time, Pallas kernels for 0%

commit v1 on v0

--- a/solution.py
+++ b/solution.py
@@ -5,6 +5,32 @@
 
 HD = 64
 EPSILON = 1e-05
+
+
+def mix_gates(mine_x, dim_i):
+    mine_x = jnp.moveaxis(mine_x, 0, dim_i)
+    block_last = mine_x.shape
+    after = mine_x.reshape(
+        *block_last[:dim_i], block_last[dim_i] * block_last[dim_i + 1], *block_last[dim_i + 2 :]
+    )
+    return after
+
+
+def spread_surface(array_in, axis_name):
+    axis_n = lax.psum(1, axis_name)
+    built = array_in[None]
+    for ix in range(axis_n.bit_length() - 1):
+        tall = 1 << ix
+        tile_out = lax.ppermute(built, axis_name, [(q, q ^ tall) for q in range(axis_n)])
+        local_now = jnp.stack([built, tile_out], axis=0)
+        seen_now = lax.axis_index(axis_name) >> ix & 1
+        built = jnp.where(seen_now == 0, local_now, local_now[::-1]).reshape(-1, *array_in.shape)
+    return built
+
+
+def find_scales_on(state, x_local, in_dim):
+    u1 = mix_gates(spread_surface(state, x_local), in_dim)
+    return u1
 
 
 def norm_scale(values):
@@ -114,7 +140,7 @@
     gate_probs = powers / jnp.sum(powers, axis=-1, keepdims=True)
     row_gates = lax.all_to_all(gate_probs.T, "wide", split_axis=0, concat_axis=0, tiled=True)
     row_gates = row_gates.reshape(-1, 1)
-    rows_in = lax.all_gather(ffn_normed, "wide", axis=0, tiled=True)
+    rows_in = find_scales_on(ffn_normed, "wide", 0)
     gate_act = jnp.dot(rows_in, full_gate[0], preferred_element_type=f32)
     up_act = jnp.dot(rows_in, full_up[0], preferred_element_type=f32)
     hidden_act = (jax.nn.silu(gate_act) * up_act).astype(bf16)

time: 1270 us -> 1630 us (1.28)
  waiting for transfers between devices: 884 us -> 1190 us
  other arithmetic: 56.7 us -> 109 us
    ppermute x0 -> x4, waiting for transfers between devices: none -> 562 us  [spread_surface(): lax.ppermute(built, axis_name, [(q, q ^ tall) for q in range(axis_n)])]
    all_gather x1, waiting for transfers between devices: 128 us -> 0.02 us  [on_device(): rows_grad = lax.all_gather(grad_out, 'wide', axis=0, tiled=True)]
    all_gather x1 -> x0, waiting for transfers between devices: 117 us -> none  [on_device(): rows_in = lax.all_gather(ffn_normed, 'wide', axis=0, tiled=True)]
    select_n x0 -> x3, other arithmetic: none -> 28.2 us  [spread_surface(): jnp.where(seen_now == 0, local_now, local_now[::-1])]
    another operation x4 -> x10, other arithmetic: 1.06 us -> 25.9 us  [the longest x6 24.9 us: spread_surface(): local_now = jnp.stack([built, tile_out], axis=0)]
    dot_general x1, matrix products: 16 us -> 32.6 us  [on_device(): gate_act = jnp.dot(rows_in, full_gate[0], preferred_element_type=f32)]
  transfers between devices with their start and end apart: 14 -> 17, of which waited for: 12 -> 12; matrix products, arithmetic and copies ran while one was open for 14% -> 14% of each run, Pallas kernels for 0% -> 0%
where the time goes in v1:
time: 1630 us
  waiting for transfers between devices  1190 us (73%)
  matrix products  257 us (16%)
  other arithmetic  109 us (7%)
  local copies, waits for them, and re-layouts  30.9 us (2%)
    ppermute x4, waiting for transfers between devices, spread_surface(): lax.ppermute(built, axis_name, [(q, q ^ tall) for q in range(axis_n)])  562 us
    reduce_scatter x1, waiting for transfers between devices, on_device(): lax.psum_scatter((row_gates * outputs.astype(f32)).astype(bf16), 'wide',...  176 us
    reduce_scatter x1, waiting for transfers between devices, on_device(): lax.psum_scatter(copy_grads, 'wide', scatter_dimension=0, tiled=True)  141 us
    psum x1, waiting for transfers between devices, on_device(): small = lax.psum(small, everywhere)  121 us
    all_gather x1, waiting for transfers between devices, on_device(): columns = lax.all_gather(shares, everywhere, axis=0, tiled=True).astype(f32)  71 us
    reduce_scatter x1, waiting for transfers between devices, on_device(): lax.psum_scatter(columns.astype(bf16), everywhere, scatter_dimension=0, t...  50.2 us
  transfers between devices with their start and end apart: 17, of which 12 were waited for; matrix products, arithmetic and copies ran while one was open for 14% of the time, Pallas kernels for 0%

profile of v1, /device:TPU:0, one launch (start us, length us, event | category | flops | bytes accessed | tf_op | source)
XLA Modules:
  0.0 1625.6 jit_solution(6333809857060032126)
XLA Ops:
  25.6 8.3 exponential_reduce_fusion
  34.9 8.7 fusion.27
  56.8 57.5 %collective-permute-done.1 = bf16[2,512,1024]{2,1,0:T(8,128)(2,1)} collective-permute-done((bf16[2,512,1024]{2,1,0:T(8,128)(2,1)}, bf16[2,512,1024]{2,1,0:T(8,128)(2,1)}, u32[]{:S(2)}, u32[]{:S(2)}) %collective-permute-start.1) | collective-permute-done | bytes 2097184 | tf_op jit(solution)/shard_map/ppermute | solution.py:24
  122.6 150.5 %collective-permute-done.2 = bf16[4,512,1024]{2,1,0:T(8,128)(2,1)} collective-permute-done((bf16[4,512,1024]{2,1,0:T(8,128)(2,1)}, bf16[4,512,1024]{2,1,0:T(8,128)(2,1)}, u32[]{:S(2)}, u32[]{:S(2)}) %collective-permute-start.2) | collective-permute-done | bytes 4194336 | tf_op jit(solution)/shard_map/ppermute | solution.py:24
  273.1 7.5 pad_maximum_fusion.1
  280.6 14.3 reverse_select_fusion.1
  305.1 353.5 %collective-permute-done.3 = bf16[8,512,1024]{2,1,0:T(8,128)(2,1)} collective-permute-done((bf16[8,512,1024]{2,1,0:T(8,128)(2,1)}, bf16[8,512,1024]{2,1,0:T(8,128)(2,1)}, u32[]{:S(2)}, u32[]{:S(2)}) %collective-permute-start.3) | collective-permute-done | bytes 8388640 | tf_op jit(solution)/shard_map/ppermute | solution.py:24
  658.5 8.0 pad_maximum_fusion
  666.5 10.7 reverse_select_fusion
  677.2 16.0 fusion.49
  693.3 16.1 fusion.9
  709.3 32.6 %multiply_convert_fusion = (bf16[8192,512]{1,0:T(8,128)(2,1)}, bf16[8192,512]{1,0:T(8,128)(2,1)}, bf16[8192,512]{1,0:T(8,128)(2,1)}) fusion(f32[8192,512]{1,0:T(8,128)} %fusion.9, f32[8192,512]{1,0:T(8,128)} %fusion.49, bf16[8192,1024]{1,0:T(8,128)(2,1)} %bitcast.179, bf16[1,1024,512]{2,1,0:T(8,128)(2,1)} %all-gather.6.cloned.1.call-done), kind=kOutput, calls=%fused_computation.15 | convolution fusion | flops 8657043456 | bytes 76546048 | tf_op jit(solution)/shard_map/dot_general | solution.py:144
  741.9 19.0 %fusion.51 = f32[8192,1024]{1,0:T(8,128)} fusion(bf16[8192,512]{1,0:T(8,128)(2,1)} %get-tuple-element.65, bf16[1,1024,512]{2,1,0:T(8,128)(2,1)} %all-gather.6.cloned.1.call-done), kind=kOutput, calls=%fused_computation.86 | convolution fusion | flops 8589934592 | bytes 42991616 | tf_op jit(solution)/shard_map/rf,df->rd/dot_general | solution.py:173
  760.9 21.5 %add_convert_fusion = bf16[8192,1024]{1,0:T(8,128)(2,1)} fusion(f32[8192,1024]{1,0:T(8,128)} %fusion.51, bf16[8192,512]{1,0:T(8,128)(2,1)} %get-tuple-element.64, bf16[1,1024,512]{2,1,0:T(8,128)(2,1)S(1)} %copy-done.61), kind=kOutput, calls=%fused_computation.6 | convolution fusion | flops 8606711808 | bytes 59768832 | tf_op jit(solution)/shard_map/rf,df->rd/dot_general | solution.py:174
  783.6 23.3 %fusion.1 = (f32[8192]{0:T(1024)S(1)}, bf16[8192,1024]{1,0:T(8,128)(2,1)}) fusion(bf16[8192,1024]{1,0:T(8,128)(2,1)} %all-gather.12.cloned.1.call-done, f32[8192]{0:T(1024)S(1)} %bitcast.208, bf16[8192,512]{1,0:T(8,128)(2,1)} %get-tuple-element.66, bf16[1,512,1024]{2,1,0:T(8,128)(2,1)S(1)} %copy-done.60), kind=kOutput, calls=%fused_computation.4 | convolution fusion | flops 8648646656 | bytes 43057152 | tf_op jit(solution)/shard_map/dot_general | solution.py:147
  807.1 11.6 all_to_all.21
  818.7 141.5 %reduce-scatter.11.cloned.1.call-done = bf16[512,1024]{1,0:T(8,128)(2,1)} async-done(((bf16[8192,1024]{1,0:T(8,128)(2,1)}), bf16[512,1024]{1,0:T(8,128)(2,1)}) %reduce-scatter.11.cloned.1.call-update) | async-done | bytes 1048592 | tf_op jit(solution)/shard_map/reduce_scatter | solution.py:176
  964.2 176.5 %reduce-scatter.9.cloned.1.call-done = bf16[512,1024]{1,0:T(8,128)(2,1)} async-done(((bf16[8192,1024]{1,0:T(8,128)(2,1)}), bf16[512,1024]{1,0:T(8,128)(2,1)}) %reduce-scatter.9.cloned.1.call-update) | async-done | bytes 1048592 | tf_op jit(solution)/shard_map/reduce_scatter | solution.py:148
  1152.3 9.4 fusion.43
  1161.7 16.0 fusion.3
  1177.7 11.1 fusion.5
  1202.6 15.1 pad_maximum_fusion.2
  1217.7 8.6 copy.93
  1226.4 15.7 fusion.34
  1242.2 16.1 fusion.33
  1258.6 18.8 %fusion.40 = bf16[1,512,1024]{2,1,0:T(8,128)(2,1)} fusion(bf16[8192,512]{1,0:T(8,128)(2,1)} %get-tuple-element.66, bf16[8192,1024]{1,0:T(8,128)(2,1)} %all-gather.12.cloned.1.call-done, f32[8192]{0:T(1024)S(1)} %bitcast.209), kind=kOutput, calls=%fused_computation.76 | convolution fusion | flops 8615624704 | bytes 26247168 | tf_op jit(solution)/shard_map/rf,rd->fd/dot_general | solution.py:164
  1290.3 50.2 %reduce-scatter.19.cloned.1.call-done = bf16[32,3072]{1,0:T(8,128)(2,1)} async-done(((bf16[1024,3072]{1,0:T(8,128)(2,1)}), bf16[32,3072]{1,0:T(8,128)(2,1)}) %reduce-scatter.19.cloned.1.call-update) | async-done | bytes 196624 | tf_op jit(solution)/shard_map/reduce_scatter | solution.py:238
  1340.5 22.3 %reduce-scatter.15.cloned.1.call-done = bf16[1,1024,256]{2,1,0:T(8,128)(2,1)} async-done(((bf16[1,1024,512]{2,1,0:T(8,128)(2,1)}), bf16[1,1024,256]{2,1,0:T(8,128)(2,1)}) %reduce-scatter.15.cloned.1.call-update) | async-done | bytes 524304 | tf_op jit(solution)/shard_map/reduce_scatter | solution.py:181
  1364.9 21.1 %reduce-scatter.13.cloned.1.call-done = bf16[1,1024,256]{2,1,0:T(8,128)(2,1)} async-done(((bf16[1,1024,512]{2,1,0:T(8,128)(2,1)}), bf16[1,1024,256]{2,1,0:T(8,128)(2,1)}) %reduce-scatter.13.cloned.1.call-update) | async-done | bytes 524304 | tf_op jit(solution)/shard_map/reduce_scatter | solution.py:178
  1388.1 21.0 %reduce-scatter.17.cloned.1.call-done = bf16[1,256,1024]{2,1,0:T(8,128)(2,1)} async-done(((bf16[1,512,1024]{2,1,0:T(8,128)(2,1)}), bf16[1,256,1024]{2,1,0:T(8,128)(2,1)}) %reduce-scatter.17.cloned.1.call-update) | async-done | bytes 524304 | tf_op jit(solution)/shard_map/reduce_scatter | solution.py:184
  1415.0 120.5 %all-reduce.2.cloned.1.call-done = f32[144,128]{1,0:T(8,128)} async-done(((f32[144,128]{1,0:T(8,128)}), f32[144,128]{1,0:T(8,128)}) %all-reduce.2.cloned.1.call-update) | async-done | bytes 73744 | tf_op jit(solution)/shard_map/psum | solution.py:240
  1538.7 71.0 %all-gather.14.cloned.1.call-done = bf16[1024,3072]{1,0:T(8,128)(2,1)} async-done(((bf16[32,3072]{1,0:T(8,128)(2,1)}), bf16[1024,3072]{1,0:T(8,128)(2,1)}) %all-gather.14.cloned.1.call-update) | async-done | bytes 6291472 | tf_op jit(solution)/shard_map/all_gather | solution.py:239
  (227 shorter events, 116.3 us)
Async XLA Ops:
  7.2 36.4 %copy-start = (bf16[1024,1024]{1,0:T(8,128)(2,1)S(1)}, bf16[1024,1024]{1,0:T(8,128)(2,1)}, u32[]{:S(2)}) copy-start(bf16[1024,1024]{1,0:T(8,128)(2,1)} %param.21) | copy-start | bytes 6291460
  7.2 670.0 %all-gather.8.cloned.1.call-start = ((), (), s32[]{:S(2)}) async-start(), calls=%async_computation.9 | async-start | bytes 1572864 | tf_op jit(solution)/shard_map/all_gather | solution.py:103
  8.0 685.3 %all-gather.10.cloned.1.call-start = ((), (), s32[]{:S(2)}) async-start(), calls=%async_computation.10 | async-start | bytes 1572864 | tf_op jit(solution)/shard_map/all_gather | solution.py:104
  8.7 684.5 %all-gather.12.cloned.1.call-start = ((), (), s32[]{:S(2)}) async-start(), calls=%async_computation.12 | async-start | bytes 17825792 | tf_op jit(solution)/shard_map/all_gather | solution.py:100
  11.7 22.3 %copy-start.52 = (f32[512]{0:T(512)}, f32[512]{0:T(512)S(1)}, u32[]{:S(2)}) copy-start(f32[512]{0:T(512)S(1)} %get-tuple-element.88) | copy-start | bytes 6148
  45.6 251.8 %copy-start.46 = (f32[512]{0:T(512)}, f32[512]{0:T(512)S(1)}, u32[]{:S(2)}) copy-start(f32[512]{0:T(512)S(1)} %get-tuple-element.90) | copy-start | bytes 6148
  46.5 3.0 collective-permute-start
  53.8 60.5 %collective-permute-start.1 = (bf16[2,512,1024]{2,1,0:T(8,128)(2,1)}, bf16[2,512,1024]{2,1,0:T(8,128)(2,1)}, u32[]{:S(2)}, u32[]{:S(2)}) collective-permute-start(bf16[2,512,1024]{2,1,0:T(8,128)(2,1)} %get-tuple-element.80), channel_id=1, source_target_pairs={{0,4},{2,6},{4,0},{6,2},{8,12},{10,14},{12,8},{14,10},{16,20},{18,... | collective-permute-start | bytes 6291464 | tf_op jit(solution)/shard_map/ppermute | solution.py:24
  120.8 152.3 %collective-permute-start.2 = (bf16[4,512,1024]{2,1,0:T(8,128)(2,1)}, bf16[4,512,1024]{2,1,0:T(8,128)(2,1)}, u32[]{:S(2)}, u32[]{:S(2)}) collective-permute-start(bf16[4,512,1024]{2,1,0:T(8,128)(2,1)} %bitcast.24), channel_id=1, source_target_pairs={{0,8},{2,10},{4,12},{6,14},{8,0},{10,2},{12,4},{14,6},{16,24},{18,... | collective-permute-start | bytes 12582920 | tf_op jit(solution)/shard_map/ppermute | solution.py:24
  294.9 363.6 %collective-permute-start.3 = (bf16[8,512,1024]{2,1,0:T(8,128)(2,1)}, bf16[8,512,1024]{2,1,0:T(8,128)(2,1)}, u32[]{:S(2)}, u32[]{:S(2)}) collective-permute-start(bf16[8,512,1024]{2,1,0:T(8,128)(2,1)} %bitcast.176), channel_id=1, source_target_pairs={{0,16},{2,18},{4,20},{6,22},{8,24},{10,26},{12,28},{14,30},{16,0},... | collective-permute-start | bytes 25165832 | tf_op jit(solution)/shard_map/ppermute | solution.py:24
  300.9 392.3 %all-to-all-start = ((f32[16,1,512]{2,1,0:T(1,128)}), f32[16,1,512]{2,1,0:T(1,128)S(1)}, u32[]{:S(2)}, u32[]{:S(2)}) async-start(f32[16,1,512]{2,1,0:T(1,128)} %copy.73), calls=%async_computation | async-start | bytes 65536 | tf_op jit(solution)/shard_map/all_to_all | solution.py:141
  304.4 404.9 %all-gather.6.cloned.1.call-start = ((), (), s32[]{:S(2)}) async-start(), calls=%async_computation.8 | async-start | bytes 1572864 | tf_op jit(solution)/shard_map/all_gather | solution.py:102
  305.0 655.2 %reduce-scatter.11.cloned.1.call-start = ((), (), s32[]{:S(2)}) async-start(), calls=%async_computation.13 | async-start | bytes 17825792 | tf_op jit(solution)/shard_map/reduce_scatter | solution.py:176
  693.2 89.3 %copy-start.50 = (f32[16,1,512]{2,1,0:T(1,128)}, f32[16,1,512]{2,1,0:T(1,128)S(1)}, u32[]{:S(2)}) copy-start(f32[16,1,512]{2,1,0:T(1,128)S(1)} %all-to-all-done) | copy-start | bytes 98308
  782.4 358.2 %reduce-scatter.9.cloned.1.call-start = ((), (), s32[]{:S(2)}) async-start(), calls=%async_computation.11 | async-start | bytes 17825792 | tf_op jit(solution)/shard_map/reduce_scatter | solution.py:148
  807.0 153.2 %copy-start.41 = (bf16[1024,16]{0,1:T(8,128)(2,1)S(1)}, bf16[1024,16]{0,1:T(8,128)(2,1)}, u32[]{:S(2)}) copy-start(bf16[1024,16]{0,1:T(8,128)(2,1)} %param.23) | copy-start | bytes 98308
  807.0 153.2 %copy-start.43 = (f32[1024]{0:T(1024)S(1)}, f32[1024]{0:T(1024)}, u32[]{:S(2)}) copy-start(f32[1024]{0:T(1024)} %param.22) | copy-start | bytes 12292
  807.0 153.2 %copy-start.47 = (f32[512]{0:T(512)S(1)}, f32[512]{0:T(512)}, u32[]{:S(2)}) copy-start(f32[512]{0:T(512)} %copy-done.46) | copy-start | bytes 6148
  807.0 333.6 %copy-start.10 = (bf16[512,1024]{1,0:T(8,128)(2,1)S(1)}, bf16[512,1024]{1,0:T(8,128)(2,1)}, u32[]{:S(2)}) copy-start(bf16[512,1024]{1,0:T(8,128)(2,1)} %param.27) | copy-start | bytes 3145732
  807.1 333.6 %copy-start.58 = (f32[512]{0:T(512)S(1)}, f32[512]{0:T(512)}, u32[]{:S(2)}) copy-start(f32[512]{0:T(512)} %get-tuple-element.89) | copy-start | bytes 6148
  807.1 533.4 %reduce-scatter.19.cloned.1.call-start = ((), (), s32[]{:S(2)}) async-start(), calls=%async_computation.19 | async-start | bytes 6488064 | tf_op jit(solution)/shard_map/reduce_scatter | solution.py:238
  818.7 326.2 %copy-start.36 = (f32[16,1,512]{2,1,0:T(1,128)}, f32[16,1,512]{2,1,0:T(1,128)S(1)}, u32[]{:S(2)}) copy-start(f32[16,1,512]{2,1,0:T(1,128)S(1)} %all_to_all.21) | copy-start | bytes 98308
  1152.3 25.4 %slice-start = ((s8[16777216]{0:T(1024)(128)(4,1)}), s8[4194304]{0:T(1024)(128)(4,1)S(1)}, s32[]{:S(2)}) async-start(s8[16777216]{0:T(1024)(128)(4,1)} %bitcast.174), calls=%async_computation.20 | async-start | bytes 8388608
  1152.3 25.4 %slice-start.1 = ((s8[16777216]{0:T(1024)(128)(4,1)}), s8[4194304]{0:T(1024)(128)(4,1)S(1)}, s32[]{:S(2)}) async-start(s8[16777216]{0:T(1024)(128)(4,1)} %bitcast.174), calls=%async_computation.21 | async-start | bytes 8388608
  1226.3 136.5 %reduce-scatter.15.cloned.1.call-start = ((), (), s32[]{:S(2)}) async-start(), calls=%async_computation.17 | async-start | bytes 1572864 | tf_op jit(solution)/shard_map/reduce_scatter | solution.py:181
  1242.1 143.9 %reduce-scatter.13.cloned.1.call-start = ((), (), s32[]{:S(2)}) async-start(), calls=%async_computation.16 | async-start | bytes 1572864 | tf_op jit(solution)/shard_map/reduce_scatter | solution.py:178
  1258.3 19.2 %copy-start.25 = (f32[512,16]{0,1:T(8,128)S(1)}, f32[512,16]{0,1:T(8,128)}, u32[]{:S(2)}) copy-start(f32[512,16]{0,1:T(8,128)} %copy-done.23) | copy-start | bytes 98308
  1258.3 19.2 %copy-start.37 = (f32[16,1,512]{2,1,0:T(1,128)S(1)}, f32[16,1,512]{2,1,0:T(1,128)}, u32[]{:S(2)}) copy-start(f32[16,1,512]{2,1,0:T(1,128)} %copy-done.36) | copy-start | bytes 98308
  1258.3 150.8 %reduce-scatter.17.cloned.1.call-start = ((), (), s32[]{:S(2)}) async-start(), calls=%async_computation.18 | async-start | bytes 1572864 | tf_op jit(solution)/shard_map/reduce_scatter | solution.py:184
  1277.4 258.2 %all-reduce.2.cloned.1.call-start = ((), (), s32[]{:S(2)}) async-start(), calls=%async_computation.14 | async-start | bytes 147456 | tf_op jit(solution)/shard_map/psum | solution.py:240
  1289.3 122.0 %copy-start.57 = (f32[512]{0:T(512)S(1)}, f32[512]{0:T(512)}, u32[]{:S(2)}) copy-start(f32[512]{0:T(512)} %get-tuple-element.87) | copy-start | bytes 6148
  1290.0 319.8 %all-gather.14.cloned.1.call-start = ((), (), s32[]{:S(2)}) async-start(), calls=%async_computation.15 | async-start | bytes 6488064 | tf_op jit(solution)/shard_map/all_gather | solution.py:239
  (51 other events, 321.5 us)
Sparse Core Ops, SparseCore 0:
  9.5 23.9 all-gather.7
  35.1 21.2 all-gather.9
  58.6 180.4 all-gather.11
  306.5 22.4 all-gather.5
  782.6 177.6 reduce-scatter.10
  964.2 176.4 reduce-scatter.8
  1226.4 114.0 reduce-scatter.18
  1343.3 19.4 reduce-scatter.14
  1365.6 20.3 reduce-scatter.12
  1388.7 20.3 reduce-scatter.16
  1415.3 120.2 all-reduce.1
  1538.3 71.3 all-gather.13
